TPU v7x, 256 devices: a whole 4x4x8 slice. The times are simulated.
256 devices in a mesh: ctx: 16 (over z_hi, x), tp: 4 (over y), dp: 4 (over z_lo, core).
Axes of the slice: x: 4, y: 4, z: 8 (z_hi: 4, z_lo: 2; z = z_hi * 2 + z_lo), core: 2. Of those that a mesh axis runs over, the one named last changes fastest.
Arguments:
- byte_embed: bfloat16 [65536, 1024], P(('dp', 'ctx', 'tp')), parts along dimension 0, may hold values from -6 to 6
- patch_start: int32 [65536], P(('dp', 'ctx', 'tp')), parts along dimension 0, may hold values from 0 to 1, as said below
- enc_gain: float32 [1024], replicated, may hold values from 0.1 to 1.9
- enc_qkv: bfloat16 [1024, 3072], replicated, may hold values from -4 to 4
- enc_out: bfloat16 [1024, 1024], replicated, may hold values from -0.1875 to 0.1875
- up_proj: bfloat16 [1024, 4096], P('ctx', 'tp'), may hold values from -0.1875 to 0.1875
- lat_gain: float32 [4096], replicated, may hold values from 0.1 to 1.9
- query_proj: bfloat16 [4096, 2048], P('ctx', 'tp'), may hold values from -4 to 4
- key_proj: bfloat16 [4096, 512], P('ctx', 'tp'), may hold values from -4 to 4
- value_matrix: bfloat16 [4096, 512], P('ctx', 'tp'), may hold values from -0.09375 to 0.09375
- out_proj: bfloat16 [2048, 4096], P('tp', 'ctx'), may hold values from -0.125 to 0.125
- down_proj: bfloat16 [4096, 1024], P('tp', 'ctx'), may hold values from -0.09375 to 0.09375
Outputs:
- byte_states: bfloat16 [65536, 1024], P(('dp', 'ctx', 'tp')), parts along dimension 0
There are 4 independent parts, one for each index of `dp`. A program takes and returns all parts, laid end to end along the dimension named above; an argument that names none is the same for every part. Nothing has to cross between parts.
Inputs may be any that keep to these rules, and one draw needn't show every extreme that they name: `patch_start`: byte 0 begins a patch; every patch spans 1 to 19 bytes; each aligned group of 1024 bytes holds at most 256 patch starts, and some group holds exactly 256.
All inputs are finite; a program needn't handle non-finite values.
Results may differ from a plain program's by a relative error of at most 0.015.
Values may be sent and summed in bfloat16 or wider, within the bound.
A program may use at most 128 MiB of HBM per device.

v0:
```python
import jax
import jax.numpy as jnp
from jax import lax
from jax.sharding import PartitionSpec as P

BH = 16
HB = 64
HEAD_SIZE = 128
WIN = 512
EPS = 1e-05


def shifted(block, axis, distance):
    devices = range(lax.axis_size(axis))
    route = [(i - distance, i) for i in devices if i - distance in devices]
    return lax.ppermute(block, axis, route)


def in_order(parts, dim):
    parts = jnp.moveaxis(parts, 0, dim)
    dims = parts.shape
    return parts.reshape(*dims[:dim], dims[dim] * dims[dim + 1], *dims[dim + 2 :])


def from_everyone(value, axis):
    copies = jnp.broadcast_to(value, (lax.axis_size(axis), *value.shape))
    return lax.all_to_all(copies, axis, split_axis=0, concat_axis=0, tiled=True)


def gathered_copies(value, axis, dim):
    return in_order(from_everyone(value, axis), dim)


def in_blocks(value, dim, peers):
    before, after = (value.shape[:dim], value.shape[dim + 1 :])
    return jnp.moveaxis(value.reshape(*before, peers, -1, *after), dim, 0)


def sum_at_owner(value, axis, dim):
    parts = in_blocks(value, dim, lax.axis_size(axis))
    arrived = lax.all_to_all(parts, axis, split_axis=0, concat_axis=0, tiled=True)
    return arrived.astype(jnp.float32).sum(axis=0)


def in_one_piece(arrays, axis, dim, along):
    columns = [a.reshape(*a.shape[:along], -1) for a in arrays]
    both = jnp.concatenate(columns, axis=along)
    result, at, gathered = (sum_at_owner(both, axis, dim), 0, [])
    for a, column in zip(arrays, columns):
        piece = result[..., at : at + column.shape[along]]
        gathered.append(piece.reshape(*piece.shape[:along], *a.shape[along:]))
        at += column.shape[along]
    return tuple(gathered)


def sent_together(arrays, axis, dim, along):
    ends, at = ([], 0)
    for a in arrays[:-1]:
        at += a.shape[along]
        ends.append(at)
    both = jnp.concatenate(arrays, axis=along)
    return tuple(jnp.split(lax.all_gather(both, axis, axis=dim, tiled=True), ends, axis=along))


def taken_together(value, axis):
    everything = from_everyone(value, axis)
    return jnp.sum(everything.astype(jnp.float32), axis=0)


def rms_scale(values, gain):
    floats = values.astype(jnp.float32)
    return floats * lax.rsqrt(jnp.mean(floats * floats, axis=-1, keepdims=True) + EPS) * gain


def window_attend(query, keys, values, first):
    n_query = query.shape[0]
    n_key = keys.shape[0]
    qh = query.reshape(n_query, BH, HB)
    kh = keys.reshape(n_key, BH, HB)
    vh = values.reshape(n_key, BH, HB)
    scores = jnp.einsum("qhd,khd->hqk", qh, kh, preferred_element_type=jnp.float32) / jnp.sqrt(
        jnp.float32(HB)
    )
    q_pos = first + jnp.arange(n_query, dtype=jnp.int32)
    k_pos = first - (n_key - n_query) + jnp.arange(n_key, dtype=jnp.int32)
    allowed = (
        (k_pos[None, :] <= q_pos[:, None])
        & (k_pos[None, :] > q_pos[:, None] - WIN)
        & (k_pos[None, :] >= 0)
    )
    scores = jnp.where(allowed[None], scores, jnp.float32(-1e30))
    peak = jnp.max(scores, axis=-1, keepdims=True)
    expo = jnp.where(allowed[None], jnp.exp(scores - peak), jnp.float32(0.0))
    total = jnp.sum(expo, axis=-1, keepdims=True)
    mixed = (
        jnp.einsum(
            "hqk,khd->hqd", expo.astype(jnp.bfloat16), vh, preferred_element_type=jnp.float32
        )
        / total
    )
    return jnp.transpose(mixed, (1, 0, 2)).reshape(n_query, BH * HB).astype(jnp.bfloat16)


def local(
    byte_embed,
    patch_start,
    enc_gain,
    enc_qkv,
    enc_out,
    up_proj,
    lat_gain,
    query_proj,
    key_proj,
    value_matrix,
    out_proj,
    down_proj,
):
    nbytes = byte_embed.shape[0]
    width = byte_embed.shape[1]
    n_tp = lax.axis_size("tp")
    n_ctx = lax.axis_size("ctx")
    device = lax.axis_index(("ctx", "tp"))
    group = device // n_tp
    slots = n_tp * nbytes // 4
    normed = rms_scale(byte_embed, enc_gain).astype(jnp.bfloat16)
    qkv = jnp.dot(normed, enc_qkv, preferred_element_type=jnp.float32).astype(jnp.bfloat16)
    query = qkv[:, :width]
    earlier = (qkv[:, width : 2 * width], qkv[:, 2 * width :])
    key_list = [earlier[0]]
    value_list = [earlier[1]]
    for step in range(2):
        earlier = shifted((earlier[0], earlier[1]), ("ctx", "tp"), 1)
        key_list.insert(0, earlier[0])
        value_list.insert(0, earlier[1])
    context = window_attend(
        query,
        jnp.concatenate(key_list, axis=0),
        jnp.concatenate(value_list, axis=0),
        device * nbytes,
    )
    hidden = (
        byte_embed.astype(jnp.float32)
        + jnp.dot(context, enc_out, preferred_element_type=jnp.float32)
    ).astype(jnp.bfloat16)
    local_count = jnp.sum(patch_start)
    all_counts = gathered_copies(local_count[None], ("ctx", "tp"), 0)
    before = jnp.cumsum(all_counts) - all_counts
    offset = before[device] - before[group * n_tp]
    group_counts = jnp.sum(all_counts.reshape(n_ctx, n_tp), axis=1)
    local_slot = jnp.cumsum(patch_start) - 1
    slot = offset + local_slot
    columns = jnp.arange(slots, dtype=jnp.int32)
    onehot = ((slot[:, None] == columns[None, :]) & (local_slot[:, None] >= 0)).astype(jnp.bfloat16)
    part_sum = jnp.dot(onehot.T, hidden, preferred_element_type=jnp.float32)
    part_count = jnp.sum(onehot.astype(jnp.float32), axis=0)
    leading = (local_slot < 0).astype(jnp.bfloat16)
    lead_sum = jnp.dot(leading[None, :], hidden, preferred_element_type=jnp.float32)
    lead_count = jnp.sum(leading.astype(jnp.float32))[None]
    recv_sum, recv_count = shifted((lead_sum, lead_count), ("ctx", "tp"), -1)
    last = offset + local_count - 1
    last_hot = (columns == last).astype(jnp.float32)
    part_sum = part_sum + last_hot[:, None] * recv_sum
    part_count = part_count + last_hot * recv_count
    sums, counts = in_one_piece(
        (part_sum.astype(jnp.bfloat16), part_count.astype(jnp.bfloat16)), "tp", 0, 1
    )
    share = (sums / jnp.maximum(counts, 1.0)[:, None]).astype(jnp.bfloat16)
    pooled = gathered_copies(share, "tp", 0)
    latent_part = jnp.dot(
        pooled,
        lax.all_gather(up_proj, "ctx", axis=0, tiled=True),
        preferred_element_type=jnp.float32,
    ).astype(jnp.bfloat16)
    latent = gathered_copies(latent_part, "tp", 1)
    lnorm = rms_scale(latent, lat_gain).astype(jnp.bfloat16)

    def proj_add(piece):
        return jnp.dot(lnorm, piece, preferred_element_type=jnp.float32)

    pieces = sent_together((query_proj, key_proj, value_matrix), "ctx", 0, 1)
    q_sum, k_sum, v_sum = tuple((proj_add(pieces[i]) for i in range(3)))
    q_local = q_sum.astype(jnp.bfloat16)
    k_local = k_sum.astype(jnp.bfloat16)
    v_local = v_sum.astype(jnp.bfloat16)
    heads_local = q_local.shape[1] // HEAD_SIZE
    kv_local = k_local.shape[1] // HEAD_SIZE
    share_count = heads_local // kv_local
    q_grouped = jnp.transpose(
        q_local.reshape(slots, kv_local, share_count, HEAD_SIZE), (1, 2, 0, 3)
    ).reshape(kv_local, share_count * slots, HEAD_SIZE)
    query_rows = group * slots + jnp.tile(jnp.arange(slots, dtype=jnp.int32), share_count)
    scale = 1.0 / jnp.sqrt(jnp.float32(HEAD_SIZE))
    peak = jnp.full((kv_local, share_count * slots), -1e30, jnp.float32)
    k_piece, v_piece = sent_together((k_local, v_local), "ctx", 0, 1)
    count = k_piece.shape[0]
    k_heads = jnp.transpose(k_piece.reshape(count, kv_local, HEAD_SIZE), (1, 0, 2))
    v_heads = jnp.transpose(v_piece.reshape(count, kv_local, HEAD_SIZE), (1, 0, 2))
    key_rows = jnp.arange(count, dtype=jnp.int32)
    used = key_rows % slots < group_counts[key_rows // slots]
    allowed = used[None, :] & (key_rows[None, :] <= query_rows[:, None])
    scores = (
        jnp.einsum("hqd,hkd->hqk", q_grouped, k_heads, preferred_element_type=jnp.float32) * scale
    )
    scores = jnp.where(allowed[None], scores, jnp.float32(-1e30))
    new_peak = jnp.maximum(peak, jnp.max(scores, axis=-1))
    expo = jnp.where(allowed[None], jnp.exp(scores - new_peak[..., None]), jnp.float32(0.0))
    total = jnp.sum(expo, axis=-1)
    accum = jnp.einsum(
        "hqk,hkd->hqd", expo.astype(jnp.bfloat16), v_heads, preferred_element_type=jnp.float32
    )
    peak, total, accum = (new_peak, total, accum)
    mixed = accum / total[..., None]
    attn = (
        jnp.transpose(mixed.reshape(kv_local, share_count, slots, HEAD_SIZE), (2, 0, 1, 3))
        .reshape(slots, heads_local * HEAD_SIZE)
        .astype(jnp.bfloat16)
    )
    partial_value = jnp.dot(
        attn,
        lax.all_gather(out_proj, "ctx", axis=1, tiled=True),
        preferred_element_type=jnp.float32,
    )
    attn_part = sum_at_owner(partial_value.astype(jnp.bfloat16), "tp", 1)
    latent_out = (latent_part.astype(jnp.float32) + attn_part).astype(jnp.bfloat16)
    down_part = jnp.dot(
        latent_out,
        lax.all_gather(down_proj, "ctx", axis=1, tiled=True),
        preferred_element_type=jnp.float32,
    )
    patch_out = (
        taken_together(down_part.astype(jnp.bfloat16), "tp")
        .astype(jnp.float32)
        .astype(jnp.bfloat16)
    )
    trailing = lax.dynamic_slice_in_dim(patch_out, last, 1, 0)
    carried = shifted(trailing, ("ctx", "tp"), 1)
    spread = jnp.dot(onehot, patch_out, preferred_element_type=jnp.float32) + leading.astype(
        jnp.float32
    )[:, None] * carried.astype(jnp.float32)
    return (hidden.astype(jnp.float32) + spread).astype(jnp.bfloat16)


def solution(mesh):
    placed = (
        P(("dp", "ctx", "tp"), None),
        P(("dp", "ctx", "tp")),
        P(),
        P(),
        P(),
        P("ctx", "tp"),
        P(),
        P("ctx", "tp"),
        P("ctx", "tp"),
        P("ctx", "tp"),
        P("tp", "ctx"),
        P("tp", "ctx"),
    )
    return jax.shard_map(
        local, mesh=mesh, in_specs=placed, out_specs=P(("dp", "ctx", "tp"), None), check_vma=False
    )
```

profile of v0, /device:TPU:64, one launch (start us, length us, event | category | flops | bytes accessed | tf_op | source)
XLA Modules:
  0.0 502.0 jit_solution(70620909785672022)
XLA Ops:
  6.5 0.7 all-gather.6.cloned.1.call-update
  7.3 1.8 pad_maximum_fusion.3
  9.1 1.4 reduce_sum.106
  10.5 1.2 broadcast_in_dim.40
  11.8 13.8 %all-to-all-start = ((s32[64,1,1]{2,1,0:T(1,128)}), s32[64,1,1]{2,1,0:T(1,128)S(1)}, u32[]{:S(2)}, u32[]{:S(2)}) async-start(s32[64,1,1]{2,1,0:T(1,128)} %broadcast_in_dim.40), calls=%async_computation | async-start | bytes 65536 | tf_op jit(solution)/shard_map/all_to_all | solution.py:27
  25.6 1.2 fusion.36
  26.8 4.9 convolution_convert_fusion.1
  31.7 0.9 fusion.72
  32.6 3.4 collective-permute-start
  36.0 3.4 collective-permute-start.2
  40.0 0.6 convert_reduce_fusion.3
  40.6 7.6 %collective-permute-start.5 = (f32[1]{0:T(128)}, f32[1]{0:T(128)}, u32[]{:S(2)}, u32[]{:S(2)}) collective-permute-start(f32[1]{0:T(128)} %bitcast.15), channel_id=1, source_target_pairs={{4,0},{8,4},{12,8},{16,12},{20,16},{24,20},{28,24},{32,28},{36,32}... | collective-permute-start | bytes 20 | tf_op jit(solution)/shard_map/ppermute | solution.py:16
  48.5 1.0 copy.45
  49.8 1.2 reduce.9
  51.0 0.7 fusion.74
  53.0 2.2 collective-permute-done
  55.2 1.9 collective-permute-start.1
  57.2 22.2 %collective-permute-done.2 = bf16[256,1024]{1,0:T(8,128)(2,1)} collective-permute-done((bf16[256,1024]{1,0:T(8,128)(2,1)S(1)}, bf16[256,1024]{1,0:T(8,128)(2,1)}, u32[]{:S(2)}, u32[]{:S(2)}) %collective-permute-start.2) | collective-permute-done | bytes 524320 | tf_op jit(solution)/shard_map/ppermute | solution.py:16
  79.4 1.9 collective-permute-start.3
  82.2 0.6 add_convert_fusion.4
  82.8 7.7 %collective-permute-done.1 = bf16[256,1024]{1,0:T(8,128)(2,1)S(1)} collective-permute-done((bf16[256,1024]{1,0:T(8,128)(2,1)}, bf16[256,1024]{1,0:T(8,128)(2,1)S(1)}, u32[]{:S(2)}, u32[]{:S(2)}) %collective-permute-start.1) | collective-permute-done | bytes 524320 | tf_op jit(solution)/shard_map/ppermute | solution.py:16
  90.5 2.5 pad_maximum_fusion
  93.0 2.6 copy.46
  95.6 5.0 collective-permute-done.3
  100.6 2.5 pad_maximum_fusion.1
  103.1 2.6 copy.47
  105.7 8.4 %fusion.75 = (f32[16,256]{1,0:T(8,128)S(1)}, bf16[16,256,768]{2,1,0:T(8,128)(2,1)}) fusion(pred[256,768]{1,0:T(8,128)(4,1)S(1)} %and_and_fusion, bf16[256,16,64]{0,2,1:T(8,128)(2,1)S(1)} %bitcast.98, bf16[768,16,64]{0,2,1:T(8,128)(2,1)} %bitcast.94), kind=kOutput, calls=%fused_computation.127 | convolution fusion | flops 421528320 | bytes 8601600 | tf_op jit(solution)/shard_map/sub | solution.py:93
  114.1 5.3 %fusion.33 = bf16[256,16,64]{0,2,1:T(8,128)(2,1)S(1)} fusion(bf16[768,16,64]{0,2,1:T(8,128)(2,1)} %bitcast.95, bf16[16,256,768]{2,1,0:T(8,128)(2,1)} %get-tuple-element.30, f32[256,16]{0,1:T(8,128)S(1)} %bitcast.111), kind=kOutput, calls=%fused_computation.41 | convolution fusion | flops 403177472 | bytes 8404992 | tf_op jit(solution)/shard_map/hqk,khd->hqd/dot_general | solution.py:96
  119.4 0.7 fusion.18
  120.3 1.9 collective-permute-start.4
  122.4 3.4 collective-permute-done.4
  125.8 0.4 add_convert_fusion.2
  126.3 10.8 %all_to_all.31 = bf16[4,64,1025]{2,1,0:T(8,128)(2,1)S(1)} all-to-all(bf16[4,64,1025]{2,1,0:T(8,128)(2,1)S(1)} %pad_maximum_fusion.2), channel_id=1, replica_groups=mesh['ctx'=16,'tp'=4,'dp'=4] {'tp'}, dimensions={0} | all-to-all | bytes 1049600 | tf_op jit(solution)/shard_map/all_to_all | solution.py:41
  137.5 10.5 %all_to_all.32 = bf16[4,64,1024]{2,1,0:T(8,128)(2,1)S(1)} all-to-all(bf16[4,64,1024]{2,1,0:T(8,128)(2,1)S(1)} %broadcast_in_dim.42), channel_id=1, replica_groups=mesh['ctx'=16,'tp'=4,'dp'=4] {'tp'}, dimensions={0} | all-to-all | bytes 1048576 | tf_op jit(solution)/shard_map/all_to_all | solution.py:27
  148.0 2.3 convolution_convert_fusion.3
  150.7 25.1 %all_to_all.33 = bf16[4,256,1024]{1,2,0:T(8,128)(2,1)S(1)} all-to-all(bf16[4,256,1024]{1,2,0:T(8,128)(2,1)S(1)} %broadcast_in_dim.43), channel_id=1, replica_groups=mesh['ctx'=16,'tp'=4,'dp'=4] {'tp'}, dimensions={0} | all-to-all | bytes 4194304 | tf_op jit(solution)/shard_map/all_to_all | solution.py:27
  175.7 0.6 multiply_reduce_fusion
  176.3 1.7 fusion.14
  178.0 46.4 %all-gather.8.cloned.1.call-done = bf16[4096,768]{1,0:T(8,128)(2,1)} async-done(((bf16[256,768]{1,0:T(8,128)(2,1)}), bf16[4096,768]{1,0:T(8,128)(2,1)}) %all-gather.8.cloned.1.call-update) | async-done | bytes 6291472 | tf_op jit(solution)/shard_map/all_gather | solution.py:62
  224.5 2.4 convolution_convert_fusion.4
  226.9 2.4 convolution_convert_fusion.5
  229.3 0.7 pad_maximum_fusion.4
  230.1 0.5 all-gather.12.cloned.1.call-update
  230.6 0.5 all-gather.14.cloned.1.call-update
  231.9 0.7 fusion.73
  232.7 4.3 compare_select_fusion.1
  237.0 5.6 %fusion.63 = pred[4096]{0:T(1024)(128)(4,1)S(1)} fusion(pred[4096]{0:T(1024)(128)(4,1)S(1)} %compare_reduce_fusion, pred[4096]{0:T(1024)(128)(4,1)S(1)} %compare_reduce_fusion.1, pred[4096]{0:T(1024)(128)(4,1)S(1)} %compare_reduce_fusion.2, pred[4096]{0:T(1024)(128)(4,1)S(1)} %compare_reduce_fusion.3, pred[4096]{0:T(1024)(128)(4,1)S(1)} %compare_reduce_fusion.4, ...), kind=kLoop, calls=%fused_computation.96 | loop fusion | flops 65536 | bytes 57380 | tf_op jit(solution)/shard_map/lt | solution.py:199
  242.6 3.4 fusion.27
  246.2 60.9 %all-gather.10.cloned.1.call-done = bf16[4096,256]{0,1:T(8,128)(2,1)} async-done(((bf16[256,256]{0,1:T(8,128)(2,1)}), bf16[4096,256]{0,1:T(8,128)(2,1)}) %all-gather.10.cloned.1.call-update) | async-done | bytes 2097168 | tf_op jit(solution)/shard_map/all_gather | solution.py:62
  307.1 6.7 %fusion.2 = (f32[1024]{0:T(1024)S(1)}, f32[1024,4096]{1,0:T(8,128)S(1)}) fusion(s32[1024]{0:T(1024)S(1)} %bitcast.105, pred[4096]{0:T(1024)(128)(4,1)S(1)} %fusion.63, bf16[1024,128]{1,0:T(8,128)(2,1)S(1)} %bitcast.102, bf16[4096,256]{0,1:T(8,128)(2,1)} %all-gather.10.cloned.1.call-done), kind=kOutput, calls=%fused_computation.5 | convolution fusion | flops 1094712320 | bytes 18100224 | tf_op jit(solution)/shard_map/hqd,hkd->hqk/dot_general | solution.py:202
  313.8 7.7 %fusion.70 = f32[1024]{0:T(1024)S(1)} fusion(f32[1024]{0:T(1024)S(1)} %broadcast_maximum_fusion, f32[1024,4096]{1,0:T(8,128)S(1)} %get-tuple-element.32, s32[1024]{0:T(1024)S(1)} %bitcast.106, pred[4096]{0:T(1024)(128)(4,1)S(1)} %fusion.63), kind=kLoop, calls=%fused_computation.123 | loop fusion | flops 29359104 | bytes 16793600 | tf_op jit(solution)/shard_map/reduce_sum | solution.py:207
  321.5 6.0 %fusion.24 = bf16[1024,128]{1,0:T(8,128)(2,1)S(1)} fusion(bf16[4096,256]{0,1:T(8,128)(2,1)S(1)} %copy-done.7, f32[1024]{0:T(1024)S(1)} %fusion.70, f32[1024,4096]{1,0:T(8,128)S(1)} %get-tuple-element.32, f32[1024]{0:T(1024)S(1)} %broadcast_maximum_fusion, s32[1024]{0:T(1024)S(1)} %bitcast.107, pred[4096]{0:T(1024)(128)(4,1)S(1)} %fusion.63), kind=kOutput, calls=%fused_computation.37 | convolution fusion | flops 1103364096 | bytes 18104320 | tf_op jit(solution)/shard_map/hqk,hkd->hqd/dot_general | solution.py:208
  327.6 61.0 %all-gather.12.cloned.1.call-done = bf16[512,4096]{1,0:T(8,128)(2,1)} async-done(((bf16[512,256]{1,0:T(8,128)(2,1)}), bf16[512,4096]{1,0:T(8,128)(2,1)}) %all-gather.12.cloned.1.call-update) | async-done | bytes 4194320 | tf_op jit(solution)/shard_map/all_gather | solution.py:220
  388.6 3.5 convolution_convert_fusion
  392.2 27.1 %all_to_all.34 = bf16[4,256,1024]{2,1,0:T(8,128)(2,1)S(1)} all-to-all(bf16[4,256,1024]{2,1,0:T(8,128)(2,1)S(1)} %bitcast.93), channel_id=1, replica_groups=mesh['ctx'=16,'tp'=4,'dp'=4] {'tp'}, dimensions={0} | all-to-all | bytes 4194304 | tf_op jit(solution)/shard_map/all_to_all | solution.py:41
  419.8 28.2 %all-gather.14.cloned.1.call-done = bf16[1024,1024]{0,1:T(8,128)(2,1)} async-done(((bf16[1024,64]{0,1:T(8,128)(2,1)}), bf16[1024,1024]{0,1:T(8,128)(2,1)}) %all-gather.14.cloned.1.call-update) | async-done | bytes 2097168 | tf_op jit(solution)/shard_map/all_gather | solution.py:227
  448.0 2.3 convolution_convert_fusion.2
  450.4 1.6 broadcast_in_dim.82
  452.0 4.4 all-to-all-start.5
  456.4 25.2 %all-to-all-done.5 = bf16[4,256,1024]{2,1,0:T(8,128)(2,1)} async-done(((bf16[4,256,1024]{2,1,0:T(8,128)(2,1)}), bf16[4,256,1024]{2,1,0:T(8,128)(2,1)}, u32[]{:S(2)}, u32[]{:S(2)}) %all-to-all-start.5) | async-done | bytes 2097184 | tf_op jit(solution)/shard_map/all_to_all | solution.py:27
  481.6 2.0 reduce_sum.115
  483.7 2.5 collective-permute-start.6
  486.2 8.1 %collective-permute-done.6 = bf16[1,1024]{1,0:T(2,128)(2,1)S(1)} collective-permute-done((bf16[1,1024]{1,0:T(2,128)(2,1)S(1)}, bf16[1,1024]{1,0:T(2,128)(2,1)S(1)}, u32[]{:S(2)}, u32[]{:S(2)}) %collective-permute-start.6) | collective-permute-done | bytes 2080 | tf_op jit(solution)/shard_map/ppermute | solution.py:16
  494.3 1.2 add_convert_fusion
  (76 shorter events, 4.2 us)
Async XLA Ops:
  6.5 112.9 %copy-start = (bf16[1024,1024]{1,0:T(8,128)(2,1)S(1)}, bf16[1024,1024]{1,0:T(8,128)(2,1)}, u32[]{:S(2)}) copy-start(bf16[1024,1024]{1,0:T(8,128)(2,1)} %param.16) | copy-start | bytes 6291460
  6.5 141.5 %all-gather.6.cloned.1.call-start = ((), (), s32[]{:S(2)}) async-start(), calls=%async_computation.6 | async-start | bytes 2228224 | tf_op jit(solution)/shard_map/all_gather | solution.py:171
  7.3 217.2 %all-gather.8.cloned.1.call-start = ((), (), s32[]{:S(2)}) async-start(), calls=%async_computation.7 | async-start | bytes 6684672 | tf_op jit(solution)/shard_map/all_gather | solution.py:62
  11.8 37.8 %all-to-all-start = ((s32[64,1,1]{2,1,0:T(1,128)}), s32[64,1,1]{2,1,0:T(1,128)S(1)}, u32[]{:S(2)}, u32[]{:S(2)}) async-start(s32[64,1,1]{2,1,0:T(1,128)} %broadcast_in_dim.40), calls=%async_computation | async-start | bytes 65536 | tf_op jit(solution)/shard_map/all_to_all | solution.py:27
  25.5 281.5 %all-gather.10.cloned.1.call-start = ((), (), s32[]{:S(2)}) async-start(), calls=%async_computation.8 | async-start | bytes 2228224 | tf_op jit(solution)/shard_map/all_gather | solution.py:62
  26.8 12.5 %copy-start.6 = (s32[256]{0:T(256)S(1)}, s32[256]{0:T(256)}, u32[]{:S(2)}) copy-start(s32[256]{0:T(256)} %param.13) | copy-start | bytes 3076
  32.6 22.6 %collective-permute-start = (bf16[256,1024]{1,0:T(8,128)(2,1)}, bf16[256,1024]{1,0:T(8,128)(2,1)}, u32[]{:S(2)}, u32[]{:S(2)}) collective-permute-start(bf16[256,1024]{1,0:T(8,128)(2,1)} %get-tuple-element.8), channel_id=1, source_target_pairs={{0,4},{4,8},{8,12},{12,16},{16,20},{20,24},{24,28},{28,32},{32,36}... | collective-permute-start | bytes 1572872 | tf_op jit(solution)/shard_map/ppermute | solution.py:16
  36.0 43.4 %collective-permute-start.2 = (bf16[256,1024]{1,0:T(8,128)(2,1)S(1)}, bf16[256,1024]{1,0:T(8,128)(2,1)}, u32[]{:S(2)}, u32[]{:S(2)}) collective-permute-start(bf16[256,1024]{1,0:T(8,128)(2,1)S(1)} %get-tuple-element.9), channel_id=1, source_target_pairs={{0,4},{4,8},{8,12},{12,16},{16,20},{20,24},{24,28},{28,32},{32,36}... | collective-permute-start | bytes 1572872 | tf_op jit(solution)/shard_map/ppermute | solution.py:16
  40.6 41.6 %collective-permute-start.5 = (f32[1]{0:T(128)}, f32[1]{0:T(128)}, u32[]{:S(2)}, u32[]{:S(2)}) collective-permute-start(f32[1]{0:T(128)} %bitcast.15), channel_id=1, source_target_pairs={{4,0},{8,4},{12,8},{16,12},{20,16},{24,20},{28,24},{32,28},{36,32}... | collective-permute-start | bytes 20 | tf_op jit(solution)/shard_map/ppermute | solution.py:16
  55.2 35.3 %collective-permute-start.1 = (bf16[256,1024]{1,0:T(8,128)(2,1)}, bf16[256,1024]{1,0:T(8,128)(2,1)S(1)}, u32[]{:S(2)}, u32[]{:S(2)}) collective-permute-start(bf16[256,1024]{1,0:T(8,128)(2,1)} %collective-permute-done), channel_id=1, source_target_pairs={{0,4},{4,8},{8,12},{12,16},{16,20},{20,24},{24,28},{28,32},{32,36}... | collective-permute-start | bytes 1572872 | tf_op jit(solution)/shard_map/ppermute | solution.py:16
  79.4 21.2 %collective-permute-start.3 = (bf16[256,1024]{1,0:T(8,128)(2,1)}, bf16[256,1024]{1,0:T(8,128)(2,1)}, u32[]{:S(2)}, u32[]{:S(2)}) collective-permute-start(bf16[256,1024]{1,0:T(8,128)(2,1)} %collective-permute-done.2), channel_id=1, source_target_pairs={{0,4},{4,8},{8,12},{12,16},{16,20},{20,24},{24,28},{28,32},{32,36}... | collective-permute-start | bytes 1572872 | tf_op jit(solution)/shard_map/ppermute | solution.py:16
  93.0 12.7 %copy-start.4 = (bf16[256,1024]{0,1:T(8,128)(2,1)S(1)}, bf16[256,1024]{0,1:T(8,128)(2,1)}, u32[]{:S(2)}) copy-start(bf16[256,1024]{0,1:T(8,128)(2,1)} %copy.45) | copy-start | bytes 1572868
  114.1 5.3 %copy-start.3 = (bf16[256,1024]{1,0:T(8,128)(2,1)S(1)}, bf16[256,1024]{1,0:T(8,128)(2,1)}, u32[]{:S(2)}) copy-start(bf16[256,1024]{1,0:T(8,128)(2,1)} %param.12) | copy-start | bytes 1572868
  120.3 5.5 %collective-permute-start.4 = (f32[1,1024]{1,0:T(1,128)S(1)}, f32[1,1024]{1,0:T(1,128)S(1)}, u32[]{:S(2)}, u32[]{:S(2)}) collective-permute-start(f32[1,1024]{1,0:T(1,128)S(1)} %fusion.76), channel_id=1, source_target_pairs={{4,0},{8,4},{12,8},{16,12},{20,16},{24,20},{28,24},{32,28},{36,32}... | collective-permute-start | bytes 12296 | tf_op jit(solution)/shard_map/ppermute | solution.py:16
  150.5 25.8 %copy-start.5 = (f32[4096]{0:T(1024)S(1)}, f32[4096]{0:T(1024)}, u32[]{:S(2)}) copy-start(f32[4096]{0:T(1024)} %param.18) | copy-start | bytes 49156
  178.0 64.6 %copy-start.2 = (bf16[256,4096]{0,1:T(8,128)(2,1)S(1)}, bf16[256,4096]{0,1:T(8,128)(2,1)}, u32[]{:S(2)}) copy-start(bf16[256,4096]{0,1:T(8,128)(2,1)} %fusion.14) | copy-start | bytes 6291460
  230.0 158.6 %all-gather.12.cloned.1.call-start = ((), (), s32[]{:S(2)}) async-start(), calls=%async_computation.9 | async-start | bytes 4456448 | tf_op jit(solution)/shard_map/all_gather | solution.py:220
  230.6 217.4 %all-gather.14.cloned.1.call-start = ((), (), s32[]{:S(2)}) async-start(), calls=%async_computation.10 | async-start | bytes 2228224 | tf_op jit(solution)/shard_map/all_gather | solution.py:227
  313.8 7.7 %copy-start.7 = (bf16[4096,256]{0,1:T(8,128)(2,1)S(1)}, bf16[4096,256]{0,1:T(8,128)(2,1)}, u32[]{:S(2)}) copy-start(bf16[4096,256]{0,1:T(8,128)(2,1)} %all-gather.10.cloned.1.call-done) | copy-start | bytes 6291460
  450.4 45.1 %copy-start.1 = (bf16[1024,1024]{1,0:T(8,128)(2,1)S(1)}, bf16[1024,1024]{1,0:T(8,128)(2,1)}, u32[]{:S(2)}) copy-start(bf16[1024,1024]{1,0:T(8,128)(2,1)} %param.16) | copy-start | bytes 6291460
  452.0 29.7 %all-to-all-start.5 = ((bf16[4,256,1024]{2,1,0:T(8,128)(2,1)}), bf16[4,256,1024]{2,1,0:T(8,128)(2,1)}, u32[]{:S(2)}, u32[]{:S(2)}) async-start(bf16[4,256,1024]{2,1,0:T(8,128)(2,1)} %broadcast_in_dim.82), calls=%async_computation.5 | async-start | bytes 4194304 | tf_op jit(solution)/shard_map/all_to_all | solution.py:27
  483.7 10.6 %collective-permute-start.6 = (bf16[1,1024]{1,0:T(2,128)(2,1)S(1)}, bf16[1,1024]{1,0:T(2,128)(2,1)S(1)}, u32[]{:S(2)}, u32[]{:S(2)}) collective-permute-start(bf16[1,1024]{1,0:T(2,128)(2,1)S(1)} %constant_dynamic-slice_fusion), channel_id=1, source_target_pairs={{0,4},{4,8},{8,12},{12,16},{16,20},{20,24},{24,28},{28,32},{32,36}... | collective-permute-start | bytes 6152 | tf_op jit(solution)/shard_map/ppermute | solution.py:16
Sparse Core Ops, SparseCore 0:
  9.8 61.1 all-gather.5
  73.4 151.0 all-gather.7
  230.1 76.9 all-gather.9
  309.3 79.2 all-gather.11
  390.9 57.1 all-gather.13
where the time goes:
time: 503 us; the launch traced here: 502 us
  waiting for transfers between devices  272 us (54%)
  blocking collectives  73.5 us (15%)
  matrix products  50.1 us (10%)
  starting transfers between devices  40.9 us (8%)
  other arithmetic  36.8 us (7%)
  between operations  15.6 us (3%)
  local copies, waits for them, and re-layouts  12.8 us (3%)
    all_gather x2, waiting for transfers between devices, sent_together(): lax.all_gather(both, axis, axis=dim, tiled=True)  107 us
    all_gather x1, waiting for transfers between devices, local(): lax.all_gather(out_proj, 'ctx', axis=1, tiled=True)  61 us
    ppermute x7, waiting for transfers between devices, shifted(): return lax.ppermute(block, axis, route)  48.8 us
    all_to_all x2, blocking collectives, sum_at_owner(): lax.all_to_all(parts, axis, split_axis=0, concat_axis=0, tiled=True)  38 us
    all_to_all x2, blocking collectives, from_everyone(): return lax.all_to_all(copies, axis, split_axis=0, concat_axis=0, tiled=True)  35.6 us
    all_gather x1, waiting for transfers between devices, local(): lax.all_gather(down_proj, 'ctx', axis=1, tiled=True)  28.2 us
    all_to_all x2, waiting for transfers between devices, from_everyone(): return lax.all_to_all(copies, axis, split_axis=0, concat_axis=0, tiled=True)  25.2 us
    ppermute x7, starting transfers between devices, shifted(): return lax.ppermute(block, axis, route)  22.5 us
  transfers between devices with their start and end apart: 14, of which 11 were waited for; matrix products, arithmetic and copies ran while one was open for 17% of the time, Pallas kernels for 0%

commit v1 on v0

--- a/solution.py
+++ b/solution.py
@@ -224,7 +224,9 @@
     latent_out = (latent_part.astype(jnp.float32) + attn_part).astype(jnp.bfloat16)
     down_part = jnp.dot(
         latent_out,
-        lax.all_gather(down_proj, "ctx", axis=1, tiled=True),
+        jnp.concatenate(
+            lax.all_to_all(jnp.stack([down_proj] * lax.axis_size("ctx")), "ctx", 0, 0), axis=1
+        ),
         preferred_element_type=jnp.float32,
     )
     patch_out = (

time: 503 us -> 535 us (1.064)
  waiting for transfers between devices: 272 us -> 291 us
  starting transfers between devices: 40.9 us -> 49.9 us
    all_to_all x0 -> x1, waiting for transfers between devices: none -> 46.2 us  [local(): lax.all_to_all(jnp.stack([down_proj] * lax.axis_size('ctx')), 'ctx', 0, 0)]
    all_gather x1 -> x0, waiting for transfers between devices: 28.2 us -> none  [local(): lax.all_gather(down_proj, 'ctx', axis=1, tiled=True)]
    all_to_all x0 -> x1, starting transfers between devices: none -> 9.03 us  [local(): lax.all_to_all(jnp.stack([down_proj] * lax.axis_size('ctx')), 'ctx', 0, 0)]
  transfers between devices with their start and end apart: 14 -> 14, of which waited for: 11 -> 11; matrix products, arithmetic and copies ran while one was open for 17% -> 16% of each run, Pallas kernels for 0% -> 0%
where the time goes in v1:
time: 535 us; the launch traced here: 534 us
  waiting for transfers between devices  291 us (54%)
  blocking collectives  74.3 us (14%)
  starting transfers between devices  49.9 us (9%)
  matrix products  49.6 us (9%)
  other arithmetic  38.5 us (7%)
  between operations  15.6 us (3%)
  local copies, waits for them, and re-layouts  15 us (3%)
    all_gather x2, waiting for transfers between devices, sent_together(): lax.all_gather(both, axis, axis=dim, tiled=True)  108 us
    all_gather x1, waiting for transfers between devices, local(): lax.all_gather(out_proj, 'ctx', axis=1, tiled=True)  61 us
    ppermute x7, waiting for transfers between devices, shifted(): return lax.ppermute(block, axis, route)  48.8 us
    all_to_all x1, waiting for transfers between devices, local(): lax.all_to_all(jnp.stack([down_proj] * lax.axis_size('ctx')), 'ctx', 0, 0)  46.2 us
    all_to_all x2, blocking collectives, sum_at_owner(): lax.all_to_all(parts, axis, split_axis=0, concat_axis=0, tiled=True)  38.7 us
    all_to_all x2, blocking collectives, from_everyone(): return lax.all_to_all(copies, axis, split_axis=0, concat_axis=0, tiled=True)  35.6 us
    all_to_all x2, waiting for transfers between devices, from_everyone(): return lax.all_to_all(copies, axis, split_axis=0, concat_axis=0, tiled=True)  25.8 us
    ppermute x7, starting transfers between devices, shifted(): return lax.ppermute(block, axis, route)  22.5 us
  transfers between devices with their start and end apart: 14, of which 11 were waited for; matrix products, arithmetic and copies ran while one was open for 16% of the time, Pallas kernels for 0%

profile of v1, /device:TPU:64, one launch (start us, length us, event | category | flops | bytes accessed | tf_op | source)
XLA Modules:
  0.0 533.8 jit_solution(14810680833382454426)
XLA Ops:
  6.5 0.7 all-gather.5.cloned.1.call-update
  7.3 1.8 pad_maximum_fusion.3
  9.1 1.4 reduce_sum.106
  10.5 1.2 broadcast_in_dim.40
  11.8 13.8 %all-to-all-start = ((s32[64,1,1]{2,1,0:T(1,128)}), s32[64,1,1]{2,1,0:T(1,128)S(1)}, u32[]{:S(2)}, u32[]{:S(2)}) async-start(s32[64,1,1]{2,1,0:T(1,128)} %broadcast_in_dim.40), calls=%async_computation | async-start | bytes 65536 | tf_op jit(solution)/shard_map/all_to_all | solution.py:27
  25.6 1.2 fusion.36
  26.8 4.9 convolution_convert_fusion.1
  31.7 0.9 fusion.72
  32.6 3.4 collective-permute-start
  36.0 3.4 collective-permute-start.2
  40.0 0.6 convert_reduce_fusion.3
  40.6 7.6 %collective-permute-start.5 = (f32[1]{0:T(128)}, f32[1]{0:T(128)}, u32[]{:S(2)}, u32[]{:S(2)}) collective-permute-start(f32[1]{0:T(128)} %bitcast.15), channel_id=1, source_target_pairs={{4,0},{8,4},{12,8},{16,12},{20,16},{24,20},{28,24},{32,28},{36,32}... | collective-permute-start | bytes 20 | tf_op jit(solution)/shard_map/ppermute | solution.py:16
  48.5 1.0 copy.46
  49.8 1.2 reduce.9
  51.0 0.7 fusion.74
  53.0 2.2 collective-permute-done
  55.2 1.9 collective-permute-start.1
  57.2 22.2 %collective-permute-done.2 = bf16[256,1024]{1,0:T(8,128)(2,1)} collective-permute-done((bf16[256,1024]{1,0:T(8,128)(2,1)S(1)}, bf16[256,1024]{1,0:T(8,128)(2,1)}, u32[]{:S(2)}, u32[]{:S(2)}) %collective-permute-start.2) | collective-permute-done | bytes 524320 | tf_op jit(solution)/shard_map/ppermute | solution.py:16
  79.4 1.9 collective-permute-start.3
  82.2 0.6 add_convert_fusion.4
  82.8 7.7 %collective-permute-done.1 = bf16[256,1024]{1,0:T(8,128)(2,1)S(1)} collective-permute-done((bf16[256,1024]{1,0:T(8,128)(2,1)}, bf16[256,1024]{1,0:T(8,128)(2,1)S(1)}, u32[]{:S(2)}, u32[]{:S(2)}) %collective-permute-start.1) | collective-permute-done | bytes 524320 | tf_op jit(solution)/shard_map/ppermute | solution.py:16
  90.5 2.5 pad_maximum_fusion
  93.0 2.6 copy.47
  95.6 5.0 collective-permute-done.3
  100.6 2.5 pad_maximum_fusion.1
  103.1 2.6 copy.48
  105.7 8.4 %fusion.75 = (f32[16,256]{1,0:T(8,128)S(1)}, bf16[16,256,768]{2,1,0:T(8,128)(2,1)}) fusion(pred[256,768]{1,0:T(8,128)(4,1)S(1)} %and_and_fusion, bf16[256,16,64]{0,2,1:T(8,128)(2,1)S(1)} %bitcast.102, bf16[768,16,64]{0,2,1:T(8,128)(2,1)} %bitcast.98), kind=kOutput, calls=%fused_computation.127 | convolution fusion | flops 421528320 | bytes 8601600 | tf_op jit(solution)/shard_map/sub | solution.py:93
  114.1 5.3 fusion.33
  119.4 0.7 fusion.18
  120.3 1.9 collective-permute-start.4
  122.4 3.4 collective-permute-done.4
  126.4 10.8 %all_to_all.36 = bf16[4,64,1025]{2,1,0:T(8,128)(2,1)S(1)} all-to-all(bf16[4,64,1025]{2,1,0:T(8,128)(2,1)S(1)} %pad_maximum_fusion.2), channel_id=1, replica_groups=mesh['ctx'=16,'tp'=4,'dp'=4] {'tp'}, dimensions={0} | all-to-all | bytes 1049600 | tf_op jit(solution)/shard_map/all_to_all | solution.py:41
  137.5 10.5 %all_to_all.37 = bf16[4,64,1024]{2,1,0:T(8,128)(2,1)S(1)} all-to-all(bf16[4,64,1024]{2,1,0:T(8,128)(2,1)S(1)} %broadcast_in_dim.42), channel_id=1, replica_groups=mesh['ctx'=16,'tp'=4,'dp'=4] {'tp'}, dimensions={0} | all-to-all | bytes 1048576 | tf_op jit(solution)/shard_map/all_to_all | solution.py:27
  148.0 2.3 convolution_convert_fusion.3
  150.6 0.6 copy-done.6
  151.3 25.1 %all_to_all.38 = bf16[4,256,1024]{1,2,0:T(8,128)(2,1)S(1)} all-to-all(bf16[4,256,1024]{1,2,0:T(8,128)(2,1)S(1)} %broadcast_in_dim.43), channel_id=1, replica_groups=mesh['ctx'=16,'tp'=4,'dp'=4] {'tp'}, dimensions={0} | all-to-all | bytes 4194304 | tf_op jit(solution)/shard_map/all_to_all | solution.py:27
  177.0 1.7 fusion.14
  178.7 45.8 %all-gather.7.cloned.1.call-done = bf16[4096,768]{1,0:T(8,128)(2,1)} async-done(((bf16[256,768]{1,0:T(8,128)(2,1)}), bf16[4096,768]{1,0:T(8,128)(2,1)}) %all-gather.7.cloned.1.call-update) | async-done | bytes 6291472 | tf_op jit(solution)/shard_map/all_gather | solution.py:62
  224.5 2.4 convolution_convert_fusion.4
  226.9 2.4 convolution_convert_fusion.5
  229.3 0.7 pad_maximum_fusion.4
  231.3 0.7 fusion.73
  232.1 4.4 compare_select_fusion.1
  236.5 5.5 %fusion.63 = pred[4096]{0:T(1024)(128)(4,1)S(1)} fusion(pred[4096]{0:T(1024)(128)(4,1)S(1)} %compare_reduce_fusion, pred[4096]{0:T(1024)(128)(4,1)S(1)} %compare_reduce_fusion.1, pred[4096]{0:T(1024)(128)(4,1)S(1)} %compare_reduce_fusion.2, pred[4096]{0:T(1024)(128)(4,1)S(1)} %compare_reduce_fusion.3, pred[4096]{0:T(1024)(128)(4,1)S(1)} %compare_reduce_fusion.4, ...), kind=kLoop, calls=%fused_computation.96 | loop fusion | flops 65536 | bytes 57380 | tf_op jit(solution)/shard_map/lt | solution.py:199
  242.0 3.4 fusion.27
  245.6 62.1 %all-gather.9.cloned.1.call-done = bf16[4096,256]{0,1:T(8,128)(2,1)} async-done(((bf16[256,256]{0,1:T(8,128)(2,1)}), bf16[4096,256]{0,1:T(8,128)(2,1)}) %all-gather.9.cloned.1.call-update) | async-done | bytes 2097168 | tf_op jit(solution)/shard_map/all_gather | solution.py:62
  307.7 6.7 %fusion.2 = (f32[1024]{0:T(1024)S(1)}, f32[1024,4096]{1,0:T(8,128)S(1)}) fusion(s32[1024]{0:T(1024)S(1)} %bitcast.109, pred[4096]{0:T(1024)(128)(4,1)S(1)} %fusion.63, bf16[1024,128]{1,0:T(8,128)(2,1)S(1)} %bitcast.106, bf16[4096,256]{0,1:T(8,128)(2,1)} %all-gather.9.cloned.1.call-done), kind=kOutput, calls=%fused_computation.5 | convolution fusion | flops 1094712320 | bytes 18100224 | tf_op jit(solution)/shard_map/hqd,hkd->hqk/dot_general | solution.py:202
  314.4 7.7 %fusion.70 = f32[1024]{0:T(1024)S(1)} fusion(f32[1024]{0:T(1024)S(1)} %broadcast_maximum_fusion, f32[1024,4096]{1,0:T(8,128)S(1)} %get-tuple-element.32, s32[1024]{0:T(1024)S(1)} %bitcast.110, pred[4096]{0:T(1024)(128)(4,1)S(1)} %fusion.63), kind=kLoop, calls=%fused_computation.123 | loop fusion | flops 29359104 | bytes 16793600 | tf_op jit(solution)/shard_map/reduce_sum | solution.py:207
  322.1 6.0 %fusion.24 = bf16[1024,128]{1,0:T(8,128)(2,1)S(1)} fusion(bf16[4096,256]{0,1:T(8,128)(2,1)S(1)} %copy-done.11, f32[1024]{0:T(1024)S(1)} %fusion.70, f32[1024,4096]{1,0:T(8,128)S(1)} %get-tuple-element.32, f32[1024]{0:T(1024)S(1)} %broadcast_maximum_fusion, s32[1024]{0:T(1024)S(1)} %bitcast.111, pred[4096]{0:T(1024)(128)(4,1)S(1)} %fusion.63), kind=kOutput, calls=%fused_computation.37 | convolution fusion | flops 1103364096 | bytes 18104320 | tf_op jit(solution)/shard_map/hqk,hkd->hqd/dot_general | solution.py:208
  328.3 61.0 %all-gather.11.cloned.1.call-done = bf16[512,4096]{1,0:T(8,128)(2,1)} async-done(((bf16[512,256]{1,0:T(8,128)(2,1)}), bf16[512,4096]{1,0:T(8,128)(2,1)}) %all-gather.11.cloned.1.call-update) | async-done | bytes 4194320 | tf_op jit(solution)/shard_map/all_gather | solution.py:220
  389.2 3.5 convolution_convert_fusion
  392.9 27.9 %all_to_all.39 = bf16[4,256,1024]{2,1,0:T(8,128)(2,1)} all-to-all(bf16[4,256,1024]{2,1,0:T(8,128)(2,1)S(1)} %bitcast.97), channel_id=1, replica_groups=mesh['ctx'=16,'tp'=4,'dp'=4] {'tp'}, dimensions={0} | all-to-all | bytes 4194304 | tf_op jit(solution)/shard_map/all_to_all | solution.py:41
  420.8 1.6 stack.2
  422.4 9.0 %all-to-all-start.5 = ((bf16[16,1024,64]{1,2,0:T(8,128)(2,1)}), bf16[16,1024,64]{1,2,0:T(8,128)(2,1)S(1)}, u32[]{:S(2)}, u32[]{:S(2)}) async-start(bf16[16,1024,64]{1,2,0:T(8,128)(2,1)} %stack.2), calls=%async_computation.5 | async-start | bytes 4194304 | tf_op jit(solution)/shard_map/all_to_all | solution.py:228
  431.5 2.1 convert_reduce_fusion
  433.5 46.2 %all-to-all-done.5 = bf16[16,1024,64]{1,2,0:T(8,128)(2,1)S(1)} async-done(((bf16[16,1024,64]{1,2,0:T(8,128)(2,1)}), bf16[16,1024,64]{1,2,0:T(8,128)(2,1)S(1)}, u32[]{:S(2)}, u32[]{:S(2)}) %all-to-all-start.5) | async-done | bytes 2097184 | tf_op jit(solution)/shard_map/all_to_all | solution.py:228
  479.8 1.8 convolution_convert_fusion.2
  481.6 1.6 broadcast_in_dim.82
  483.2 4.4 all-to-all-start.6
  487.6 25.8 %all-to-all-done.6 = bf16[4,256,1024]{2,1,0:T(8,128)(2,1)} async-done(((bf16[4,256,1024]{2,1,0:T(8,128)(2,1)}), bf16[4,256,1024]{2,1,0:T(8,128)(2,1)}, u32[]{:S(2)}, u32[]{:S(2)}) %all-to-all-start.6) | async-done | bytes 2097184 | tf_op jit(solution)/shard_map/all_to_all | solution.py:27
  513.4 2.0 reduce_sum.115
  515.4 2.5 collective-permute-start.6
  517.9 8.1 %collective-permute-done.6 = bf16[1,1024]{1,0:T(2,128)(2,1)S(1)} collective-permute-done((bf16[1,1024]{1,0:T(2,128)(2,1)S(1)}, bf16[1,1024]{1,0:T(2,128)(2,1)S(1)}, u32[]{:S(2)}, u32[]{:S(2)}) %collective-permute-start.6) | collective-permute-done | bytes 2080 | tf_op jit(solution)/shard_map/ppermute | solution.py:16
  526.1 1.2 add_convert_fusion
  (84 shorter events, 5.4 us)
Async XLA Ops:
  6.5 112.9 %copy-start = (bf16[1024,1024]{1,0:T(8,128)(2,1)S(1)}, bf16[1024,1024]{1,0:T(8,128)(2,1)}, u32[]{:S(2)}) copy-start(bf16[1024,1024]{1,0:T(8,128)(2,1)} %param.16) | copy-start | bytes 6291460
  6.5 141.5 %all-gather.5.cloned.1.call-start = ((), (), s32[]{:S(2)}) async-start(), calls=%async_computation.7 | async-start | bytes 2228224 | tf_op jit(solution)/shard_map/all_gather | solution.py:171
  7.3 217.2 %all-gather.7.cloned.1.call-start = ((), (), s32[]{:S(2)}) async-start(), calls=%async_computation.8 | async-start | bytes 6684672 | tf_op jit(solution)/shard_map/all_gather | solution.py:62
  11.8 37.8 %all-to-all-start = ((s32[64,1,1]{2,1,0:T(1,128)}), s32[64,1,1]{2,1,0:T(1,128)S(1)}, u32[]{:S(2)}, u32[]{:S(2)}) async-start(s32[64,1,1]{2,1,0:T(1,128)} %broadcast_in_dim.40), calls=%async_computation | async-start | bytes 65536 | tf_op jit(solution)/shard_map/all_to_all | solution.py:27
  25.5 282.2 %all-gather.9.cloned.1.call-start = ((), (), s32[]{:S(2)}) async-start(), calls=%async_computation.9 | async-start | bytes 2228224 | tf_op jit(solution)/shard_map/all_gather | solution.py:62
  26.8 12.5 %copy-start.10 = (s32[256]{0:T(256)S(1)}, s32[256]{0:T(256)}, u32[]{:S(2)}) copy-start(s32[256]{0:T(256)} %param.13) | copy-start | bytes 3076
  32.6 22.6 %collective-permute-start = (bf16[256,1024]{1,0:T(8,128)(2,1)}, bf16[256,1024]{1,0:T(8,128)(2,1)}, u32[]{:S(2)}, u32[]{:S(2)}) collective-permute-start(bf16[256,1024]{1,0:T(8,128)(2,1)} %get-tuple-element.8), channel_id=1, source_target_pairs={{0,4},{4,8},{8,12},{12,16},{16,20},{20,24},{24,28},{28,32},{32,36}... | collective-permute-start | bytes 1572872 | tf_op jit(solution)/shard_map/ppermute | solution.py:16
  36.0 43.4 %collective-permute-start.2 = (bf16[256,1024]{1,0:T(8,128)(2,1)S(1)}, bf16[256,1024]{1,0:T(8,128)(2,1)}, u32[]{:S(2)}, u32[]{:S(2)}) collective-permute-start(bf16[256,1024]{1,0:T(8,128)(2,1)S(1)} %get-tuple-element.9), channel_id=1, source_target_pairs={{0,4},{4,8},{8,12},{12,16},{16,20},{20,24},{24,28},{28,32},{32,36}... | collective-permute-start | bytes 1572872 | tf_op jit(solution)/shard_map/ppermute | solution.py:16
  40.6 41.6 %collective-permute-start.5 = (f32[1]{0:T(128)}, f32[1]{0:T(128)}, u32[]{:S(2)}, u32[]{:S(2)}) collective-permute-start(f32[1]{0:T(128)} %bitcast.15), channel_id=1, source_target_pairs={{4,0},{8,4},{12,8},{16,12},{20,16},{24,20},{28,24},{32,28},{36,32}... | collective-permute-start | bytes 20 | tf_op jit(solution)/shard_map/ppermute | solution.py:16
  55.2 35.3 %collective-permute-start.1 = (bf16[256,1024]{1,0:T(8,128)(2,1)}, bf16[256,1024]{1,0:T(8,128)(2,1)S(1)}, u32[]{:S(2)}, u32[]{:S(2)}) collective-permute-start(bf16[256,1024]{1,0:T(8,128)(2,1)} %collective-permute-done), channel_id=1, source_target_pairs={{0,4},{4,8},{8,12},{12,16},{16,20},{20,24},{24,28},{28,32},{32,36}... | collective-permute-start | bytes 1572872 | tf_op jit(solution)/shard_map/ppermute | solution.py:16
  79.4 21.2 %collective-permute-start.3 = (bf16[256,1024]{1,0:T(8,128)(2,1)}, bf16[256,1024]{1,0:T(8,128)(2,1)}, u32[]{:S(2)}, u32[]{:S(2)}) collective-permute-start(bf16[256,1024]{1,0:T(8,128)(2,1)} %collective-permute-done.2), channel_id=1, source_target_pairs={{0,4},{4,8},{8,12},{12,16},{16,20},{20,24},{24,28},{28,32},{32,36}... | collective-permute-start | bytes 1572872 | tf_op jit(solution)/shard_map/ppermute | solution.py:16
  93.0 12.7 %copy-start.7 = (bf16[256,1024]{0,1:T(8,128)(2,1)S(1)}, bf16[256,1024]{0,1:T(8,128)(2,1)}, u32[]{:S(2)}) copy-start(bf16[256,1024]{0,1:T(8,128)(2,1)} %copy.46) | copy-start | bytes 1572868
  114.1 5.3 copy-start.3
  120.2 30.2 %copy-start.4 = (bf16[256,1024]{1,0:T(8,128)(2,1)}, bf16[256,1024]{1,0:T(8,128)(2,1)S(1)}, u32[]{:S(2)}) copy-start(bf16[256,1024]{1,0:T(8,128)(2,1)S(1)} %fusion.18) | copy-start | bytes 1572868
  120.3 5.5 %collective-permute-start.4 = (f32[1,1024]{1,0:T(1,128)S(1)}, f32[1,1024]{1,0:T(1,128)S(1)}, u32[]{:S(2)}, u32[]{:S(2)}) collective-permute-start(f32[1,1024]{1,0:T(1,128)S(1)} %fusion.76), channel_id=1, source_target_pairs={{4,0},{8,4},{12,8},{16,12},{20,16},{24,20},{28,24},{32,28},{36,32}... | collective-permute-start | bytes 12296 | tf_op jit(solution)/shard_map/ppermute | solution.py:16
  150.3 0.8 copy-start.6
  151.2 25.8 %copy-start.9 = (f32[4096]{0:T(1024)S(1)}, f32[4096]{0:T(1024)}, u32[]{:S(2)}) copy-start(f32[4096]{0:T(1024)} %param.18) | copy-start | bytes 49156
  178.7 63.3 %copy-start.2 = (bf16[256,4096]{0,1:T(8,128)(2,1)S(1)}, bf16[256,4096]{0,1:T(8,128)(2,1)}, u32[]{:S(2)}) copy-start(bf16[256,4096]{0,1:T(8,128)(2,1)} %fusion.14) | copy-start | bytes 6291460
  230.0 159.2 %all-gather.11.cloned.1.call-start = ((), (), s32[]{:S(2)}) async-start(), calls=%async_computation.10 | async-start | bytes 4456448 | tf_op jit(solution)/shard_map/all_gather | solution.py:220
  314.4 7.7 %copy-start.11 = (bf16[4096,256]{0,1:T(8,128)(2,1)S(1)}, bf16[4096,256]{0,1:T(8,128)(2,1)}, u32[]{:S(2)}) copy-start(bf16[4096,256]{0,1:T(8,128)(2,1)} %all-gather.9.cloned.1.call-done) | copy-start | bytes 6291460
  392.7 28.1 %copy-start.8 = (bf16[1024,64]{0,1:T(8,128)(2,1)S(1)}, bf16[1024,64]{0,1:T(8,128)(2,1)}, u32[]{:S(2)}) copy-start(bf16[1024,64]{0,1:T(8,128)(2,1)} %param.23) | copy-start | bytes 393220
  422.4 57.3 %all-to-all-start.5 = ((bf16[16,1024,64]{1,2,0:T(8,128)(2,1)}), bf16[16,1024,64]{1,2,0:T(8,128)(2,1)S(1)}, u32[]{:S(2)}, u32[]{:S(2)}) async-start(bf16[16,1024,64]{1,2,0:T(8,128)(2,1)} %stack.2), calls=%async_computation.5 | async-start | bytes 4194304 | tf_op jit(solution)/shard_map/all_to_all | solution.py:228
  481.6 44.5 %copy-start.5 = (bf16[256,1024]{1,0:T(8,128)(2,1)S(1)}, bf16[256,1024]{1,0:T(8,128)(2,1)}, u32[]{:S(2)}) copy-start(bf16[256,1024]{1,0:T(8,128)(2,1)} %copy-done.4) | copy-start | bytes 1572868
  481.6 45.7 %copy-start.1 = (bf16[1024,1024]{1,0:T(8,128)(2,1)S(1)}, bf16[1024,1024]{1,0:T(8,128)(2,1)}, u32[]{:S(2)}) copy-start(bf16[1024,1024]{1,0:T(8,128)(2,1)} %param.16) | copy-start | bytes 6291460
  483.2 30.2 %all-to-all-start.6 = ((bf16[4,256,1024]{2,1,0:T(8,128)(2,1)}), bf16[4,256,1024]{2,1,0:T(8,128)(2,1)}, u32[]{:S(2)}, u32[]{:S(2)}) async-start(bf16[4,256,1024]{2,1,0:T(8,128)(2,1)} %broadcast_in_dim.82), calls=%async_computation.6 | async-start | bytes 4194304 | tf_op jit(solution)/shard_map/all_to_all | solution.py:27
  515.4 10.6 %collective-permute-start.6 = (bf16[1,1024]{1,0:T(2,128)(2,1)S(1)}, bf16[1,1024]{1,0:T(2,128)(2,1)S(1)}, u32[]{:S(2)}, u32[]{:S(2)}) collective-permute-start(bf16[1,1024]{1,0:T(2,128)(2,1)S(1)} %constant_dynamic-slice_fusion), channel_id=1, source_target_pairs={{0,4},{4,8},{8,12},{12,16},{16,20},{20,24},{24,28},{28,32},{32,36}... | collective-permute-start | bytes 6152 | tf_op jit(solution)/shard_map/ppermute | solution.py:16
Sparse Core Ops, SparseCore 0:
  9.8 61.1 all-gather.4
  73.4 151.0 all-gather.6
  230.1 77.5 all-gather.8
  310.0 79.2 all-gather.10
